TPU v7x, 32 devices: a whole 2x2x4 slice. The times are simulated.
32 devices in a mesh: row: 4 (over y, x), col: 8 (over z, core).
Axes of the slice: x: 2, y: 2, z: 4, core: 2. Of those that a mesh axis runs over, the one named last changes fastest.
Arguments:
- gains: float32 [512, 8, 256], P(('row', 'col')), may hold values from -6 to 6
- coherency: bfloat16 [512, 512, 8, 1, 256], P('row', 'col'), may hold values from -6 to 6
- cotangent: bfloat16 [512, 512, 8, 1, 8], P('row', 'col'), may hold values from -0.099609375 to 0.099609375
- flags: int32 [512, 512, 1], P('row', 'col'), may hold values 0 or 1
- station_slot: int32 [512], replicated, may hold values from 0 to 511, as said below
Outputs:
- gain_grad: float32 [512, 8, 256], P(('row', 'col'))
Inputs may be any that keep to these rules, and one draw needn't show every extreme that they name: `station_slot`: each station appears in exactly one slot; in every aligned block of 16 consecutive slots the stations lie with 16 different holders, station s being held by the device of index s // 16 in the order of row+col.
All inputs are finite; a program needn't handle non-finite values. No bound on the sum of `flags` on one device may be relied on, other than what follows from the above.
Results may differ from a plain program's by a relative error of at most 0.0003.
Values sent between devices are 32-bit elements; how exact they have to be, the bound alone decides.
A program may use at most 128 MiB of HBM per device.

v0:
```python
import functools

import jax
import jax.numpy as jnp
from jax import lax
from jax.experimental import pallas as pl
from jax.experimental.pallas import tpu as pltpu
from jax.sharding import PartitionSpec as P


def swap_pairs(values, width, even):
    return jnp.where(even, pltpu.roll(values, 3 * width, 1), pltpu.roll(values, width, 1))


def two_parts(values):
    high = values.astype(jnp.bfloat16)
    return high, (values - high.astype(jnp.float32)).astype(jnp.bfloat16)


def row_weights(gains, width, even, sign):
    lanes = 4 * width
    rows = []
    for b in range(2):
        half = gains[:, b * lanes : (b + 1) * lanes]
        rows += [half, -sign * swap_pairs(half, width, even)]
    tables = []
    for part in two_parts(jnp.concatenate(rows, axis=0)):
        zero = jnp.zeros_like(part)
        tables += [
            jnp.concatenate([part, zero], axis=1),
            jnp.concatenate([zero, part], axis=1),
        ]
    return jnp.concatenate(tables, axis=0)


def col_weights(gains, width, even, sign, group):
    lanes = 4 * width
    blocks = []
    for b in range(2):
        half = gains[:, b * lanes : (b + 1) * lanes]
        other = pltpu.roll(half, 2 * width, 1)
        rows = [[], []]
        for e in range(2):
            twice = jnp.where(group // 2 == e, half, other)
            rows[0].append(sign * twice)
            rows[1].append(swap_pairs(twice, width, even))
        blocks.append(
            jnp.concatenate([jnp.concatenate(row, axis=1) for row in rows], axis=0)
        )
    tables = []
    for part in range(2):
        for b in range(2):
            value = two_parts(blocks[b])[part]
            zero = jnp.zeros_like(value)
            tables += [
                jnp.concatenate([value, zero], axis=1),
                jnp.concatenate([zero, value], axis=1),
            ]
    return jnp.concatenate(tables, axis=0)


def gradient_kernel(
    width, m_ref, gt_ref, jr_ref, jc_ref, r_ref, c_ref,
    wr_ref, wc_ref, xr_ref, xa_ref, xb_ref, acc_ref,
):
    block, second, channels, _ = m_ref.shape
    lanes = 4 * width
    depth = gt_ref.shape[2]
    pair = xa_ref.shape[0]
    chunk = xa_ref.shape[1] // channels
    chunks = second // chunk
    step = pl.program_id(0)

    lane_f = lax.broadcasted_iota(jnp.int32, (channels, depth), 1) % channels
    sub_f = lax.broadcasted_iota(jnp.int32, (channels, depth), 0)
    diagonal = (lane_f == sub_f).astype(jnp.float32)
    group = lax.broadcasted_iota(jnp.int32, (channels, lanes), 1) // width
    even = group % 2 == 0
    sign = jnp.where(even, 1.0, -1.0)

    @pl.when(step == 0)
    def _():
        acc_ref[...] = jnp.zeros_like(acc_ref)

        def prepare(k, carry):
            wr_ref[k] = row_weights(jc_ref[k], width, even, sign)
            return carry

        lax.fori_loop(0, second, prepare, 0)

    def spread(rows):
        count = rows.shape[0]
        wide = rows * diagonal[None]
        return wide.reshape(count * channels, depth).astype(jnp.bfloat16)

    def row_products(k, carry):
        xr_ref[k] = jnp.dot(
            spread(gt_ref[k][:, None, :]), wr_ref[k], preferred_element_type=jnp.float32
        )
        return carry

    lax.fori_loop(0, second, row_products, 0, unroll=4)

    def stations(pair_index, carry):
        first = pair_index * pair
        for p in range(pair):
            wc_ref[p] = col_weights(jr_ref[first + p], width, even, sign, group)

        def col_products(at, x_ref):
            start = pl.multiple_of(at * chunk, chunk)
            for p in range(pair):
                x_ref[p] = jnp.dot(
                    spread(gt_ref[pl.ds(start, chunk), pl.ds(first + p, 1)]),
                    wc_ref[p],
                    preferred_element_type=jnp.float32,
                )

        def combine(at, x_ref, totals):
            totals = list(totals)
            for q in range(chunk):
                k = at * chunk + q
                col = [acc_ref[k, n] for n in range(4)]
                for p in range(pair):
                    m = m_ref[first + p, k].astype(jnp.float32)
                    halves = [m[:, :lanes], m[:, lanes:]]
                    swapped = [swap_pairs(h, width, even) for h in halves]
                    start = pl.multiple_of((first + p) * channels, channels)
                    for a in range(2):
                        x = xr_ref[k, pl.ds(start, channels), a * lanes : (a + 1) * lanes]
                        for c in range(2):
                            n = p * 8 + 4 * a + 2 * c
                            totals[n] = totals[n] + x * halves[c]
                            totals[n + 1] = totals[n + 1] + x * swapped[c]
                    for a in range(2):
                        for e in range(2):
                            n = 2 * a + e
                            y = x_ref[
                                p,
                                q * channels : (q + 1) * channels,
                                n * lanes : (n + 1) * lanes,
                            ]
                            col[2 * a] = col[2 * a] + y * halves[e]
                            col[2 * a + 1] = col[2 * a + 1] + y * swapped[e]
                for n in range(4):
                    acc_ref[k, n] = col[n]
            return tuple(totals)

        def two_chunks(j, totals):
            col_products(2 * j + 1, xb_ref)
            totals = combine(2 * j, xa_ref, totals)
            col_products(jnp.minimum(2 * j + 2, chunks - 1), xa_ref)
            return combine(2 * j + 1, xb_ref, totals)

        zero = jnp.zeros((channels, lanes), jnp.float32)
        col_products(0, xa_ref)
        totals = lax.fori_loop(0, chunks // 2, two_chunks, (zero,) * (8 * pair))
        for p in range(pair):
            for a in range(2):
                parts = []
                for n in range(4):
                    value = totals[8 * p + 4 * a + n]
                    if n % 2 == 1:
                        value = -sign * value
                    value = value + pltpu.roll(value, 2 * width, 1)
                    parts.append(value + pltpu.roll(value, width, 1))
                r_ref[first + p, :, a * lanes : (a + 1) * lanes] = jnp.where(
                    group < 2,
                    jnp.where(even, parts[0], parts[1]),
                    jnp.where(even, parts[2], parts[3]),
                )
        return carry

    lax.fori_loop(0, block // pair, stations, 0)

    @pl.when(step == pl.num_programs(0) - 1)
    def _():
        def finish(k, carry):
            for a in range(2):
                real = acc_ref[k, 2 * a]
                imag = acc_ref[k, 2 * a + 1] * sign
                real = real + swap_pairs(real, width, even)
                imag = imag + swap_pairs(imag, width, even)
                c_ref[k, :, a * lanes : (a + 1) * lanes] = jnp.where(even, real, imag)
            return carry

        lax.fori_loop(0, second, finish, 0, unroll=2)


def residuals(cotangent, flags):
    first, second, channels = cotangent.shape[:3]
    weighted = cotangent[:, :, :, 0].astype(jnp.float32) * flags.astype(jnp.float32)[..., None]
    lane_order = weighted.transpose(1, 0, 3, 2).reshape(second, first, 8 * channels)
    return jnp.concatenate([lane_order, lane_order], axis=-1)


def block_gradients(coherency, across, row_gains, col_gains):
    first, second, channels, _, wide = coherency.shape
    width = wide // 8
    block = min(32, first)
    pair = 2
    chunk = min(16, second // 2)
    depth = across.shape[2]
    model = coherency.reshape(first, second, channels, wide)
    products = (pair, chunk * channels, 2 * wide)
    return pl.pallas_call(
        functools.partial(gradient_kernel, width),
        grid=(first // block,),
        in_specs=[
            pl.BlockSpec((block, second, channels, wide), lambda s: (s, 0, 0, 0)),
            pl.BlockSpec((second, block, depth), lambda s: (0, s, 0)),
            pl.BlockSpec((block, channels, wide), lambda s: (s, 0, 0)),
            pl.BlockSpec((second, channels, wide), lambda s: (0, 0, 0)),
        ],
        out_specs=[
            pl.BlockSpec((block, channels, wide), lambda s: (s, 0, 0)),
            pl.BlockSpec((second, channels, wide), lambda s: (0, 0, 0)),
        ],
        out_shape=[
            jax.ShapeDtypeStruct((first, channels, wide), jnp.float32),
            jax.ShapeDtypeStruct((second, channels, wide), jnp.float32),
        ],
        scratch_shapes=[
            pltpu.VMEM((second, depth, wide), jnp.bfloat16),
            pltpu.VMEM((pair, depth, 2 * wide), jnp.bfloat16),
            pltpu.VMEM((second, block * channels, wide), jnp.float32),
            pltpu.VMEM(products, jnp.float32),
            pltpu.VMEM(products, jnp.float32),
            pltpu.VMEM((second, 4, channels, wide // 2), jnp.float32),
        ],
        compiler_params=pltpu.CompilerParams(
            dimension_semantics=("arbitrary",), vmem_limit_bytes=58 * 1024 * 1024
        ),
    )(model, across, row_gains, col_gains)


MESH = pl.DeviceIdType.MESH


def device(place, col_total):
    return (place // col_total, place % col_total)


def remote(source, target, send_sem, recv_sem, where):
    return pltpu.make_async_remote_copy(
        src_ref=source,
        dst_ref=target,
        send_sem=send_sem,
        recv_sem=recv_sem,
        device_id=where,
        device_id_type=MESH,
    )


def each(start, stop, action):
    def body(index, carry):
        action(index)
        return carry

    lax.fori_loop(start, stop, body, 0)


def greet(me, total, col_total):
    barrier = pltpu.get_barrier_semaphore()

    def hello(offset):
        pl.semaphore_signal(
            barrier,
            inc=1,
            device_id=device(lax.rem(me + offset, total), col_total),
            device_id_type=MESH,
        )

    each(1, total, hello)
    pl.semaphore_wait(barrier, total - 1)


def exchange(send_ref, recv_ref, send_sems, recv_sems, me, total, col_total):
    def copy(offset):
        place = lax.rem(me + offset, total)
        return remote(
            send_ref.at[place],
            recv_ref.at[me],
            send_sems.at[offset],
            recv_sems.at[offset],
            device(place, col_total),
        )

    each(1, total, lambda offset: copy(offset).start())
    recv_ref[me] = send_ref[me]
    each(1, total, lambda offset: copy(offset).wait())


def spread_kernel(
    row_total, col_total, holders_ref, send_ref, row_ref, col_ref,
    recv_ref, x_send, x_recv, c_send, c_recv, a_send, a_recv, b_send, b_recv,
):
    share = holders_ref.shape[1]
    r = lax.axis_index("row")
    c = lax.axis_index("col")
    total = row_total * col_total
    me = r * col_total + c
    greet(me, total, col_total)
    exchange(send_ref, recv_ref, x_send, x_recv, me, total, col_total)

    def choose(j):
        row_ref[c * share + j] = recv_ref[holders_ref[0, j], 0]
        col_ref[r * share + j] = recv_ref[holders_ref[1, j], 1]

    each(0, share, choose)
    half = col_total // 2
    partner = c + 1 - 2 * (c % 2)

    def col_copy(offset):
        block = col_ref.at[pl.ds(r * share, share)]
        where = (lax.rem(r + offset, row_total), c)
        return remote(block, block, c_send.at[offset], c_recv.at[offset], where)

    def far_copy(offset):
        block = row_ref.at[pl.ds(c * share, share)]
        where = (r, lax.rem(c + 2 * offset, col_total))
        return remote(block, block, a_send.at[offset], a_recv.at[offset], where)

    def near_copy(offset):
        origin = lax.rem(c + col_total - 2 * offset, col_total)
        block = row_ref.at[pl.ds(origin * share, share)]
        return remote(block, block, b_send.at[offset], b_recv.at[offset], (r, partner))

    each(1, half, lambda offset: far_copy(offset).start())
    each(1, row_total, lambda offset: col_copy(offset).start())
    near_copy(0).start()

    def forward(offset):
        far_copy(offset).wait_recv()
        near_copy(offset).start()

    each(1, half, forward)
    each(1, half, lambda offset: far_copy(offset).wait_send())
    each(0, half, lambda offset: near_copy(offset).wait())
    each(1, row_total, lambda offset: col_copy(offset).wait())


def collect_kernel(
    row_total, col_total, back_ref, own_ref, row_ref, col_ref, out_ref,
    pair_ref, part_ref, far_ref, colin_ref, sums_ref, send_ref, recv_ref,
    x_send, x_recv, c_send, c_recv, a_send, a_recv, b_send, b_recv,
):
    share = own_ref.shape[1]
    r = lax.axis_index("row")
    c = lax.axis_index("col")
    total = row_total * col_total
    me = r * col_total + c
    half = col_total // 2
    core = c % 2
    chip = c // 2
    greet(me, total, col_total)

    def near_copy(offset):
        q = lax.rem(chip + offset, half)
        block = row_ref.at[pl.ds((2 * q + 1 - core) * share, share)]
        return remote(
            block, pair_ref.at[q], a_send.at[offset], a_recv.at[offset], (r, 2 * chip + 1 - core)
        )

    def far_copy(offset):
        q = lax.rem(chip + offset, half)
        return remote(
            part_ref.at[q], far_ref.at[offset], b_send.at[offset], b_recv.at[offset],
            (r, 2 * q + core),
        )

    def col_copy(offset):
        there = lax.rem(r + offset, row_total)
        block = col_ref.at[pl.ds(there * share, share)]
        return remote(
            block, colin_ref.at[offset], c_send.at[offset], c_recv.at[offset], (there, c)
        )

    def join(offset):
        near_copy(offset).wait_recv()
        q = lax.rem(chip + offset, half)
        part_ref[q] = row_ref[pl.ds((2 * q + core) * share, share)] + pair_ref[q]

    def join_and_send(offset):
        join(offset)
        far_copy(offset).start()

    each(1, half + 1, lambda offset: near_copy(lax.rem(offset, half)).start())
    each(1, row_total, lambda offset: col_copy(offset).start())
    each(1, half, join_and_send)
    join(0)
    sums_ref[0] = part_ref[chip]
    sums_ref[1] = col_ref[pl.ds(r * share, share)]

    def add_col(offset):
        col_copy(offset).wait()
        sums_ref[1] += colin_ref[offset]

    def add_row(offset):
        far_copy(offset).wait()
        sums_ref[0] += far_ref[offset]

    each(1, row_total, add_col)
    each(1, half, add_row)
    each(0, half, lambda offset: near_copy(offset).wait_send())

    def address(place):
        send_ref[place, 0] = sums_ref[0, back_ref[0, place]]
        send_ref[place, 1] = sums_ref[1, back_ref[1, place]]

    each(0, total, address)
    exchange(send_ref, recv_ref, x_send, x_recv, me, total, col_total)

    def settle(j):
        out_ref[j] = recv_ref[own_ref[0, j], 0] + recv_ref[own_ref[1, j], 1]

    each(0, share, settle)


def semaphores(total, row_total, col_total):
    counts = (total, row_total, col_total // 2, col_total // 2)
    return [pltpu.SemaphoreType.DMA((count,)) for count in counts for _ in range(2)]


def places(identifiers, count):
    here = identifiers[:, None] == jnp.arange(count, dtype=jnp.int32)[None, :]
    index = jnp.arange(identifiers.shape[0], dtype=jnp.int32)[:, None]
    return jnp.sum(jnp.where(here, index, 0), axis=0, dtype=jnp.int32)


def call_options(identifier):
    return pltpu.CompilerParams(collective_id=identifier, has_side_effects=True)


def shards(gains, coherency, cotangent, flags, station_slot):
    stations = station_slot.shape[0]
    share = gains.shape[0]
    tail = gains.shape[1:]
    row_total = lax.axis_size("row")
    col_total = lax.axis_size("col")
    groups = row_total * col_total
    row_place = lax.axis_index("row")
    col_place = lax.axis_index("col")
    device_place = row_place * col_total + col_place
    counting = jnp.arange(share, dtype=jnp.int32)
    mine = device_place * share + counting
    found = station_slot[None, :] == mine[:, None]
    slot_index = jnp.arange(stations, dtype=jnp.int32)[None, :]
    own_blocks = jnp.sum(jnp.where(found, slot_index, 0), axis=1, dtype=jnp.int32) // share
    col_target = own_blocks % row_total * col_total + own_blocks // row_total
    col_block = col_place * row_total + row_place
    row_holder = lax.dynamic_slice_in_dim(station_slot, device_place * share, share) // share
    col_holder = lax.dynamic_slice_in_dim(station_slot, col_block * share, share) // share
    holders = jnp.stack([row_holder, col_holder])
    targets = jnp.stack([own_blocks, col_target])
    picks = jnp.stack([places(own_blocks, groups), places(col_target, groups)], axis=1)
    sent = jnp.take(gains, picks.reshape(-1), axis=0).reshape((groups, 2) + tail)
    vmem = pl.BlockSpec(memory_space=pltpu.VMEM)
    smem = pl.BlockSpec(memory_space=pltpu.SMEM)
    f32 = jnp.float32
    table = pltpu.VMEM((groups, 2) + tail, f32)
    row_gains, col_gains = pl.pallas_call(
        functools.partial(spread_kernel, row_total, col_total),
        in_specs=[smem, vmem],
        out_specs=[vmem, vmem],
        out_shape=[
            jax.ShapeDtypeStruct((col_total * share,) + tail, f32),
            jax.ShapeDtypeStruct((row_total * share,) + tail, f32),
        ],
        scratch_shapes=[table] + semaphores(groups, row_total, col_total),
        compiler_params=call_options(1),
    )(holders, sent)
    row_side, col_side = block_gradients(
        coherency, residuals(cotangent, flags), row_gains, col_gains
    )
    backs = jnp.stack([places(row_holder, groups), places(col_holder, groups)])
    half = col_total // 2
    return pl.pallas_call(
        functools.partial(collect_kernel, row_total, col_total),
        in_specs=[smem, smem, vmem, vmem],
        out_specs=vmem,
        out_shape=jax.ShapeDtypeStruct(gains.shape, f32),
        scratch_shapes=[
            pltpu.VMEM((half, share) + tail, f32),
            pltpu.VMEM((half, share) + tail, f32),
            pltpu.VMEM((half, share) + tail, f32),
            pltpu.VMEM((row_total, share) + tail, f32),
            pltpu.VMEM((2, share) + tail, f32),
            table,
            table,
        ]
        + semaphores(groups, row_total, col_total),
        compiler_params=call_options(2),
    )(backs, targets, row_side, col_side)


def solution(mesh):
    placed = (
        P(("row", "col"), None, None),
        P("row", "col", None, None, None),
        P("row", "col", None, None, None),
        P("row", "col", None),
        P(),
    )
    return jax.shard_map(
        shards, mesh=mesh, in_specs=placed, out_specs=P(("row", "col"), None, None), check_vma=False
    )
```

profile of v0, /device:TPU:0, one launch (start us, length us, event | category | flops | bytes accessed | tf_op | source)
XLA Modules:
  0.0 211.2 jit_solution(16846646598862149445)
XLA Ops:
  0.0 0.0 copy-start
  0.0 0.8 and_select_fusion.7
  0.8 0.1 select_reduce_fusion.3
  0.9 0.6 pad_add_fusion.back_ref
  1.5 0.9 select_reduce_fusion
  2.4 0.5 pad_add_fusion.1.own_ref
  2.9 0.8 convert_element_type.11
  3.7 1.5 fusion
  5.3 2.7 %copy.15 = f32[64,128,64]{2,1,0:T(8,128)} copy(f32[64,128,64]{1,2,0:T(8,128)S(1)} %fusion) | data formatting | bytes 4194304 | tf_op jit(solution)/shard_map/reshape | solution.py:192
  8.0 6.5 %pad_maximum_fusion.gt_ref = f32[64,128,128]{2,1,0:T(8,128)} fusion(f32[64,128,64]{2,1,0:T(8,128)} %copy.15), kind=kLoop, calls=%fused_computation.1 | loop fusion | flops 1048576 | bytes 6291456 | tf_op jit(solution)/shard_map/concatenate | solution.py:193
  14.6 0.6 pad_add_fusion.2.holders_ref
  15.2 0.1 select_reduce_fusion.1
  15.3 0.1 copy.18
  15.4 0.1 reshape.228
  15.5 0.0 copy-done
  15.5 0.6 gather_fusion
  16.2 0.1 copy.17
  16.3 0.9 broadcast_select_fusion.send_ref
  17.2 35.5 %shard_map.55 = (f32[128,8,256]{2,1,0:T(8,128)}, f32[64,8,256]{2,1,0:T(8,128)}) custom-call(s32[2,16]{1,0:T(2,128)} %pad_add_fusion.2.holders_ref, f32[32,2,8,256]{3,2,1,0:T(8,128)} %broadcast_select_fusion.send_ref), custom_call_target="tpu_custom_call" | custom-call | tf_op jit(solution)/shard_map/pallas_call | solution.py:461
  52.7 123.3 %shard_map.56 = (f32[128,8,256]{2,1,0:T(8,128)}, f32[64,8,256]{2,1,0:T(8,128)}) custom-call(bf16[128,64,8,256]{3,2,1,0:T(8,128)(2,1)} %bitcast.28, f32[64,128,128]{2,1,0:T(8,128)} %pad_maximum_fusion.gt_ref, f32[128,8,256]{2,1,0:T(8,128)} %get-tuple-element.9.jr_ref, f32[64,8,256]{2,1,0:T(8,128)} %get-tuple-element.10.jc_ref), custom_call_target="tpu_custom_call" | custom-call | tf_op jit(solution)/shard_map/pallas_call | solution.py:205
  176.0 33.6 %shard_map.57 = f32[16,8,256]{2,1,0:T(8,128)} custom-call(s32[2,32]{1,0:T(2,128)} %pad_add_fusion.back_ref, s32[2,16]{1,0:T(2,128)} %pad_add_fusion.1.own_ref, f32[128,8,256]{2,1,0:T(8,128)} %get-tuple-element.11.row_ref, f32[64,8,256]{2,1,0:T(8,128)} %get-tuple-element.12.col_ref), custom_call_target="tpu_custom_call" | custom-call | tf_op jit(solution)/shard_map/pallas_call | solution.py:477
  209.6 1.6 copy.21
  (7 shorter events, 0.1 us)
Async XLA Ops:
  0.0 15.5 %copy-start = (f32[16,8,256]{2,1,0:T(8,128)S(1)}, f32[16,8,256]{2,1,0:T(8,128)}, u32[]{:S(2)}) copy-start(f32[16,8,256]{2,1,0:T(8,128)} %param.5) | copy-start | bytes 393220
where the time goes:
time: 212 us; the launch traced here: 211 us
  Pallas kernels  192 us (91%)
  other arithmetic  13.5 us (6%)
  local copies, waits for them, and re-layouts  5.24 us (2%)
    pallas_call x1, Pallas kernels, block_gradients(): pl.pallas_call(functools.partial(gradient_kernel, width), grid=(first //...  123 us
    pallas_call x1, Pallas kernels, shards(): pl.pallas_call(functools.partial(spread_kernel, row_total, col_total), in...  35.5 us
    pallas_call x1, Pallas kernels, shards(): pl.pallas_call(functools.partial(collect_kernel, row_total, col_total), i...  33.6 us
    concatenate x1, other arithmetic, residuals(): return jnp.concatenate([lane_order, lane_order], axis=-1)  6.54 us

commit v1 on v0

--- a/solution.py
+++ b/solution.py
@@ -60,16 +60,23 @@
 
 
 def gradient_kernel(
-    width, m_ref, gt_ref, jr_ref, jc_ref, r_ref, c_ref,
-    wr_ref, wc_ref, xr_ref, xa_ref, xb_ref, acc_ref,
+    width, block, tile, parts, m_ref, g_ref, jr_ref, jc_ref, r_ref, c_ref,
+    m_buf, m_sem, gt_ref, wr_ref, wc_ref, sxa_ref, sxb_ref, sya_ref, syb_ref,
+    xa_ref, xb_ref, ya_ref, yb_ref, acc_ref, racc_ref,
 ):
-    block, second, channels, _ = m_ref.shape
+    first, channels = jr_ref.shape[:2]
+    second = jc_ref.shape[0]
     lanes = 4 * width
     depth = gt_ref.shape[2]
-    pair = xa_ref.shape[0]
-    chunk = xa_ref.shape[1] // channels
-    chunks = second // chunk
-    step = pl.program_id(0)
+    slots = m_buf.shape[0]
+    ring = wc_ref.shape[0]
+    tiles = second // tile
+    blocks = first // block
+    total = blocks * tiles
+    rows_each = block // parts
+    cols_each = tile // parts
+    each = block // (tiles * parts)
+    early = 4
 
     lane_f = lax.broadcasted_iota(jnp.int32, (channels, depth), 1) % channels
     sub_f = lax.broadcasted_iota(jnp.int32, (channels, depth), 0)
@@ -77,56 +84,81 @@
     group = lax.broadcasted_iota(jnp.int32, (channels, lanes), 1) // width
     even = group % 2 == 0
     sign = jnp.where(even, 1.0, -1.0)
-
-    @pl.when(step == 0)
-    def _():
-        acc_ref[...] = jnp.zeros_like(acc_ref)
-
-        def prepare(k, carry):
-            wr_ref[k] = row_weights(jc_ref[k], width, even, sign)
-            return carry
-
-        lax.fori_loop(0, second, prepare, 0)
-
-    def spread(rows):
-        count = rows.shape[0]
-        wide = rows * diagonal[None]
-        return wide.reshape(count * channels, depth).astype(jnp.bfloat16)
-
-    def row_products(k, carry):
-        xr_ref[k] = jnp.dot(
-            spread(gt_ref[k][:, None, :]), wr_ref[k], preferred_element_type=jnp.float32
+    both = lax.broadcasted_iota(jnp.int32, (2 * channels, lanes), 1) // width
+    even_both = both % 2 == 0
+
+    def fetch(at):
+        row = at // tiles * block
+        col = at % tiles * tile
+        return pltpu.make_async_copy(
+            m_ref.at[pl.ds(row, block), pl.ds(col, tile)],
+            m_buf.at[at % slots],
+            m_sem.at[at % slots],
         )
-        return carry
-
-    lax.fori_loop(0, second, row_products, 0, unroll=4)
-
-    def stations(pair_index, carry):
-        first = pair_index * pair
-        for p in range(pair):
-            wc_ref[p] = col_weights(jr_ref[first + p], width, even, sign, group)
-
-        def col_products(at, x_ref):
-            start = pl.multiple_of(at * chunk, chunk)
-            for p in range(pair):
-                x_ref[p] = jnp.dot(
-                    spread(gt_ref[pl.ds(start, chunk), pl.ds(first + p, 1)]),
-                    wc_ref[p],
-                    preferred_element_type=jnp.float32,
-                )
-
-        def combine(at, x_ref, totals):
-            totals = list(totals)
-            for q in range(chunk):
-                k = at * chunk + q
+
+    def table(at):
+        return col_weights(jr_ref[at], width, even, sign, group)
+
+    def places_of(at):
+        at = jnp.minimum(at, total - 1)
+        return at // tiles * block, at % tiles * tile
+
+    def spread(at, j, sx_ref, sy_ref):
+        row, col = places_of(at)
+        for v in range(0, cols_each, 2):
+            kk = j * cols_each + v
+            for u in range(0, block, 2):
+                wide = [
+                    [
+                        gt_ref[col + kk + z, pl.ds(row + u + w, 1)] * diagonal
+                        for w in range(2)
+                    ]
+                    for z in range(2)
+                ]
+                for z in range(2):
+                    pair = jnp.concatenate(wide[z], axis=0).astype(jnp.bfloat16)
+                    sx_ref[kk + z, u * channels : (u + 2) * channels] = pair
+                    pair = jnp.concatenate([wide[0][z], wide[1][z]], axis=0)
+                    start = pl.multiple_of(kk * channels, 2 * channels)
+                    sy_ref[u + z, pl.ds(start, 2 * channels)] = pair.astype(jnp.bfloat16)
+
+    def products(at, j, sx_ref, sy_ref, x_ref, y_ref):
+        row, col = places_of(at)
+        for n in range(cols_each):
+            kk = j * cols_each + n
+            x_ref[kk] = jnp.dot(
+                sx_ref[kk], wr_ref[col + kk], preferred_element_type=jnp.float32
+            )
+        for n in range(rows_each):
+            ii = j * rows_each + n
+            y_ref[ii] = jnp.dot(
+                sy_ref[ii], wc_ref[(row + ii) % ring], preferred_element_type=jnp.float32
+            )
+
+    def combine(at, j, x_ref, y_ref):
+        pair = 2
+        slot = at % slots
+        col_at = at % tiles * tile
+        for half in range(rows_each // pair):
+            base = j * rows_each + half * pair
+            totals = [racc_ref[base + p, n] for p in range(pair) for n in range(8)]
+            for q in range(tile):
+                k = col_at + q
                 col = [acc_ref[k, n] for n in range(4)]
                 for p in range(pair):
-                    m = m_ref[first + p, k].astype(jnp.float32)
-                    halves = [m[:, :lanes], m[:, lanes:]]
-                    swapped = [swap_pairs(h, width, even) for h in halves]
-                    start = pl.multiple_of((first + p) * channels, channels)
+                    m = m_buf[slot, base + p, q]
+                    turned = jnp.where(
+                        even_both,
+                        pltpu.roll(m, 3 * width, 1),
+                        pltpu.roll(m, width, 1),
+                    )
+                    wide = m.astype(jnp.float32)
+                    halves = [wide[:channels], wide[channels:]]
+                    wide = turned.astype(jnp.float32)
+                    swapped = [wide[:channels], wide[channels:]]
+                    start = pl.multiple_of((base + p) * channels, channels)
                     for a in range(2):
-                        x = xr_ref[k, pl.ds(start, channels), a * lanes : (a + 1) * lanes]
+                        x = x_ref[q, pl.ds(start, channels), a * lanes : (a + 1) * lanes]
                         for c in range(2):
                             n = p * 8 + 4 * a + 2 * c
                             totals[n] = totals[n] + x * halves[c]
@@ -134,8 +166,8 @@
                     for a in range(2):
                         for e in range(2):
                             n = 2 * a + e
-                            y = x_ref[
-                                p,
+                            y = y_ref[
+                                base + p,
                                 q * channels : (q + 1) * channels,
                                 n * lanes : (n + 1) * lanes,
                             ]
@@ -143,94 +175,158 @@
                             col[2 * a + 1] = col[2 * a + 1] + y * swapped[e]
                 for n in range(4):
                     acc_ref[k, n] = col[n]
-            return tuple(totals)
-
-        def two_chunks(j, totals):
-            col_products(2 * j + 1, xb_ref)
-            totals = combine(2 * j, xa_ref, totals)
-            col_products(jnp.minimum(2 * j + 2, chunks - 1), xa_ref)
-            return combine(2 * j + 1, xb_ref, totals)
-
-        zero = jnp.zeros((channels, lanes), jnp.float32)
-        col_products(0, xa_ref)
-        totals = lax.fori_loop(0, chunks // 2, two_chunks, (zero,) * (8 * pair))
-        for p in range(pair):
+            for p in range(pair):
+                for n in range(8):
+                    racc_ref[base + p, n] = totals[8 * p + n]
+
+    for at in range(min(slots - 1, total)):
+        fetch(at).start()
+    acc_ref[...] = jnp.zeros_like(acc_ref)
+
+    def turn(k, carry):
+        rows = [g_ref[k, pl.ds(p, channels, stride=8)] for p in range(8)]
+        gt_ref[k] = jnp.concatenate(rows * 2, axis=0).T
+        return carry
+
+    lax.fori_loop(0, second, turn, 0, unroll=4)
+
+    def prepare(k, carry):
+        wr_ref[k] = row_weights(jc_ref[k], width, even, sign)
+        return carry
+
+    lax.fori_loop(0, second, prepare, 0, unroll=8)
+
+    def prepare_col(i, carry):
+        wc_ref[i] = table(i)
+        return carry
+
+    lax.fori_loop(0, block + early, prepare_col, 0, unroll=4)
+
+    def begin_spread(j, carry):
+        spread(0, j, sxa_ref, sya_ref)
+        spread(1, j, sxb_ref, syb_ref)
+        return carry
+
+    lax.fori_loop(0, parts, begin_spread, 0)
+
+    def begin(j, carry):
+        products(0, j, sxa_ref, sya_ref, xa_ref, ya_ref)
+        return carry
+
+    lax.fori_loop(0, parts, begin, 0)
+
+    def phase(at, here, there):
+        sx_here, sy_here, x_here, y_here = here
+        sx_there, sy_there, x_there, y_there = there
+        fetch(at).wait()
+
+        @pl.when(at + slots - 1 < total)
+        def _():
+            fetch(at + slots - 1).start()
+
+        def body(j, carry):
+            products(at + 1, j, sx_there, sy_there, x_there, y_there)
+            combine(at, j, x_here, y_here)
+            spread(at + 2, j, sx_here, sy_here)
+            step = at // tiles + 1
+            for n in range(each):
+                ahead = step * block + early + (at % tiles * parts + j) * each + n
+                wc_ref[ahead % ring] = table(jnp.minimum(ahead, first - 1))
+            return carry
+
+        lax.fori_loop(0, parts, body, 0)
+
+    a_side = (sxa_ref, sya_ref, xa_ref, ya_ref)
+    b_side = (sxb_ref, syb_ref, xb_ref, yb_ref)
+
+    def row_block(step, carry):
+        racc_ref[...] = jnp.zeros_like(racc_ref)
+
+        def two_tiles(t, carry):
+            at = step * tiles + 2 * t
+            phase(at, a_side, b_side)
+            phase(at + 1, b_side, a_side)
+            return carry
+
+        lax.fori_loop(0, tiles // 2, two_tiles, 0)
+
+        def settle(i, carry):
             for a in range(2):
-                parts = []
-                for n in range(4):
-                    value = totals[8 * p + 4 * a + n]
-                    if n % 2 == 1:
-                        value = -sign * value
-                    value = value + pltpu.roll(value, 2 * width, 1)
-                    parts.append(value + pltpu.roll(value, width, 1))
-                r_ref[first + p, :, a * lanes : (a + 1) * lanes] = jnp.where(
-                    group < 2,
-                    jnp.where(even, parts[0], parts[1]),
-                    jnp.where(even, parts[2], parts[3]),
+                values = [racc_ref[i, 4 * a + n] for n in range(4)]
+                values = [v if n % 2 == 0 else -sign * v for n, v in enumerate(values)]
+                sums = []
+                for n in (0, 2):
+                    kept = jnp.where(even, values[n], values[n + 1])
+                    moved = jnp.where(even, values[n + 1], values[n])
+                    sums.append(kept + pltpu.roll(moved, width, 1))
+                kept = jnp.where(group < 2, sums[0], sums[1])
+                moved = jnp.where(group < 2, sums[1], sums[0])
+                r_ref[step * block + i, :, a * lanes : (a + 1) * lanes] = (
+                    kept + pltpu.roll(moved, 2 * width, 1)
                 )
-        return carry
-
-    lax.fori_loop(0, block // pair, stations, 0)
-
-    @pl.when(step == pl.num_programs(0) - 1)
-    def _():
-        def finish(k, carry):
-            for a in range(2):
-                real = acc_ref[k, 2 * a]
-                imag = acc_ref[k, 2 * a + 1] * sign
-                real = real + swap_pairs(real, width, even)
-                imag = imag + swap_pairs(imag, width, even)
-                c_ref[k, :, a * lanes : (a + 1) * lanes] = jnp.where(even, real, imag)
             return carry
 
-        lax.fori_loop(0, second, finish, 0, unroll=2)
+        lax.fori_loop(0, block, settle, 0, unroll=8)
+        return carry
+
+    lax.fori_loop(0, blocks, row_block, 0)
+
+    def finish(k, carry):
+        for a in range(2):
+            real = acc_ref[k, 2 * a]
+            imag = acc_ref[k, 2 * a + 1] * sign
+            kept = jnp.where(even, real, imag)
+            moved = jnp.where(even, imag, real)
+            c_ref[k, :, a * lanes : (a + 1) * lanes] = kept + swap_pairs(moved, width, even)
+        return carry
+
+    lax.fori_loop(0, second, finish, 0, unroll=8)
 
 
 def residuals(cotangent, flags):
     first, second, channels = cotangent.shape[:3]
-    weighted = cotangent[:, :, :, 0].astype(jnp.float32) * flags.astype(jnp.float32)[..., None]
-    lane_order = weighted.transpose(1, 0, 3, 2).reshape(second, first, 8 * channels)
-    return jnp.concatenate([lane_order, lane_order], axis=-1)
-
-
-def block_gradients(coherency, across, row_gains, col_gains):
+    kept = flags.astype(jnp.float32)[..., None]
+    weighted = cotangent[:, :, :, 0].astype(jnp.float32) * kept
+    return weighted.transpose(1, 2, 3, 0).reshape(second, 8 * channels, first)
+
+
+def block_gradients(coherency, residual, row_gains, col_gains):
     first, second, channels, _, wide = coherency.shape
     width = wide // 8
-    block = min(32, first)
-    pair = 2
-    chunk = min(16, second // 2)
-    depth = across.shape[2]
-    model = coherency.reshape(first, second, channels, wide)
-    products = (pair, chunk * channels, 2 * wide)
+    lanes = wide // 2
+    block = 16
+    tile = 16
+    parts = 4
+    slots = 4
+    depth = 16 * channels
+    f32, bf16 = jnp.float32, jnp.bfloat16
+    model = coherency.reshape(first, second, channels, 2, lanes).transpose(0, 1, 3, 2, 4)
+    model = model.reshape(first, second, 2 * channels, lanes)
+    spread_x = pltpu.VMEM((tile, block * channels, depth), bf16)
+    spread_y = pltpu.VMEM((block, tile * channels, depth), bf16)
+    x_shape = pltpu.VMEM((tile, block * channels, wide), f32)
+    y_shape = pltpu.VMEM((block, tile * channels, 2 * wide), f32)
+    vmem = pl.BlockSpec(memory_space=pltpu.VMEM)
     return pl.pallas_call(
-        functools.partial(gradient_kernel, width),
-        grid=(first // block,),
-        in_specs=[
-            pl.BlockSpec((block, second, channels, wide), lambda s: (s, 0, 0, 0)),
-            pl.BlockSpec((second, block, depth), lambda s: (0, s, 0)),
-            pl.BlockSpec((block, channels, wide), lambda s: (s, 0, 0)),
-            pl.BlockSpec((second, channels, wide), lambda s: (0, 0, 0)),
-        ],
-        out_specs=[
-            pl.BlockSpec((block, channels, wide), lambda s: (s, 0, 0)),
-            pl.BlockSpec((second, channels, wide), lambda s: (0, 0, 0)),
-        ],
+        functools.partial(gradient_kernel, width, block, tile, parts),
+        in_specs=[pl.BlockSpec(memory_space=pl.ANY), vmem, vmem, vmem],
+        out_specs=[vmem, vmem],
         out_shape=[
-            jax.ShapeDtypeStruct((first, channels, wide), jnp.float32),
-            jax.ShapeDtypeStruct((second, channels, wide), jnp.float32),
+            jax.ShapeDtypeStruct((first, channels, wide), f32),
+            jax.ShapeDtypeStruct((second, channels, wide), f32),
         ],
         scratch_shapes=[
-            pltpu.VMEM((second, depth, wide), jnp.bfloat16),
-            pltpu.VMEM((pair, depth, 2 * wide), jnp.bfloat16),
-            pltpu.VMEM((second, block * channels, wide), jnp.float32),
-            pltpu.VMEM(products, jnp.float32),
-            pltpu.VMEM(products, jnp.float32),
-            pltpu.VMEM((second, 4, channels, wide // 2), jnp.float32),
+            pltpu.VMEM((slots, block, tile, 2 * channels, lanes), bf16),
+            pltpu.SemaphoreType.DMA((slots,)),
+            pltpu.VMEM((second, first, depth), f32),
+            pltpu.VMEM((second, depth, wide), bf16),
+            pltpu.VMEM((2 * block, depth, 2 * wide), bf16),
+            spread_x, spread_x, spread_y, spread_y, x_shape, x_shape, y_shape, y_shape,
+            pltpu.VMEM((second, 4, channels, lanes), f32),
+            pltpu.VMEM((block, 8, channels, lanes), f32),
         ],
-        compiler_params=pltpu.CompilerParams(
-            dimension_semantics=("arbitrary",), vmem_limit_bytes=58 * 1024 * 1024
-        ),
-    )(model, across, row_gains, col_gains)
+        compiler_params=pltpu.CompilerParams(vmem_limit_bytes=58 * 1024 * 1024),
+    )(model, residual, row_gains, col_gains)
 
 
 MESH = pl.DeviceIdType.MESH

time: 212 us -> 151 us (0.71)
  Pallas kernels: 192 us -> 142 us
  other arithmetic: 13.5 us -> 5.64 us
  local copies, waits for them, and re-layouts: 5.24 us -> 2.51 us
    pallas_call x1, Pallas kernels: 123 us -> 73.2 us  [block_gradients(): pl.pallas_call(functools.partial(gradient_kernel, width, block, tile, par...]
    concatenate x1 -> x0, other arithmetic: 6.54 us -> none  [residuals(): return jnp.concatenate([lane_order, lane_order], axis=-1)]
    reshape x1 -> x0, local copies, waits for them, and re-layouts: 2.74 us -> none  [residuals(): weighted.transpose(1, 0, 3, 2).reshape(second, first, 8 * channels)]
where the time goes in v1:
time: 151 us
  Pallas kernels  142 us (94%)
  other arithmetic  5.64 us (4%)
  local copies, waits for them, and re-layouts  2.51 us (2%)
    pallas_call x1, Pallas kernels, block_gradients(): pl.pallas_call(functools.partial(gradient_kernel, width, block, tile, par...  73.2 us
    pallas_call x1, Pallas kernels, shards(): pl.pallas_call(functools.partial(spread_kernel, row_total, col_total), in...  35.5 us
    pallas_call x1, Pallas kernels, shards(): pl.pallas_call(functools.partial(collect_kernel, row_total, col_total), i...  33.6 us

profile of v1, /device:TPU:0, one launch (start us, length us, event | category | flops | bytes accessed | tf_op | source)
XLA Modules:
  0.0 150.6 jit_solution(3180068630445227672)
XLA Ops:
  0.0 0.0 copy-start
  0.0 0.0 copy-start.3
  0.0 0.0 copy-start.2
  0.0 0.0 copy-start.1
  0.0 1.0 select_reduce_fusion
  1.0 0.1 select_reduce_fusion.1
  1.1 0.1 copy.11
  1.2 0.1 reshape.232
  1.3 0.0 copy-done
  1.4 0.6 gather_fusion
  2.0 0.1 copy.10
  2.1 0.9 broadcast_select_fusion.send_ref
  3.0 0.0 copy-done.3
  3.0 0.1 and_select_fusion.7
  3.1 0.6 pad_add_fusion.2.holders_ref
  3.7 35.5 %shard_map.55 = (f32[128,8,256]{2,1,0:T(8,128)}, f32[64,8,256]{2,1,0:T(8,128)}) custom-call(s32[2,16]{1,0:T(2,128)} %pad_add_fusion.2.holders_ref, f32[32,2,8,256]{3,2,1,0:T(8,128)} %broadcast_select_fusion.send_ref), custom_call_target="tpu_custom_call" | custom-call | tf_op jit(solution)/shard_map/pallas_call | solution.py:557
  39.2 0.0 copy-done.2
  39.3 0.0 copy-done.1
  39.3 1.7 %fusion.g_ref = f32[64,64,128]{2,1,0:T(8,128)} fusion(bf16[128,64,8,1,8]{0,4,3,2,1:T(8,128)(2,1)S(1)} %copy-done.1, f32[128,64]{0,1:T(8,128)S(1)} %bitcast.34), kind=kLoop, calls=%fused_computation.2 | loop fusion | flops 1048576 | bytes 3178496 | tf_op jit(solution)/shard_map/reshape | solution.py:290
  41.0 73.2 %shard_map.56 = (f32[128,8,256]{2,1,0:T(8,128)}, f32[64,8,256]{2,1,0:T(8,128)}) custom-call(bf16[128,64,16,128]{3,2,1,0:T(8,128)(2,1)} %bitcast.32, f32[64,64,128]{2,1,0:T(8,128)} %fusion.g_ref, f32[128,8,256]{2,1,0:T(8,128)} %get-tuple-element.9.jr_ref, f32[64,8,256]{2,1,0:T(8,128)} %get-tuple-element.10.jc_ref), custom_call_target="tpu_custom_call" | custom-call | tf_op jit(solution)/shard_map/pallas_call | solution.py:310
  114.2 0.1 select_reduce_fusion.3
  114.3 0.6 pad_add_fusion.back_ref
  114.9 0.5 pad_add_fusion.1.own_ref
  115.4 33.6 %shard_map.57 = f32[16,8,256]{2,1,0:T(8,128)} custom-call(s32[2,32]{1,0:T(2,128)} %pad_add_fusion.back_ref, s32[2,16]{1,0:T(2,128)} %pad_add_fusion.1.own_ref, f32[128,8,256]{2,1,0:T(8,128)} %get-tuple-element.11.row_ref, f32[64,8,256]{2,1,0:T(8,128)} %get-tuple-element.12.col_ref), custom_call_target="tpu_custom_call" | custom-call | tf_op jit(solution)/shard_map/pallas_call | solution.py:573
  149.1 1.6 %copy.13 = f32[16,8,256]{2,1,0:T(8,128)} copy(f32[16,8,256]{2,1,0:T(8,128)} %shard_map.57) | data formatting | bytes 262144
  (8 shorter events, 0.1 us)
Async XLA Ops:
  0.0 1.3 copy-start
  0.0 3.0 %copy-start.3 = (s32[512]{0:T(512)S(1)}, s32[512]{0:T(512)}, u32[]{:S(2)}) copy-start(s32[512]{0:T(512)} %param.9) | copy-start | bytes 6148
  0.0 39.2 %copy-start.2 = (s32[128,64,1]{0,2,1:T(1,128)S(1)}, s32[128,64,1]{0,2,1:T(1,128)}, u32[]{:S(2)}) copy-start(s32[128,64,1]{0,2,1:T(1,128)} %param.8) | copy-start | bytes 98308
  0.0 39.3 %copy-start.1 = (bf16[128,64,8,1,8]{0,4,3,2,1:T(8,128)(2,1)S(1)}, bf16[128,64,8,1,8]{0,4,3,2,1:T(8,128)(2,1)}, u32[]{:S(2)}) copy-start(bf16[128,64,8,1,8]{0,4,3,2,1:T(8,128)(2,1)} %param.7) | copy-start | bytes 3145732

commit v2 on v1

--- a/solution.py
+++ b/solution.py
@@ -188,7 +188,7 @@
         gt_ref[k] = jnp.concatenate(rows * 2, axis=0).T
         return carry
 
-    lax.fori_loop(0, second, turn, 0, unroll=4)
+    lax.fori_loop(0, second, turn, 0, unroll=8)
 
     def prepare(k, carry):
         wr_ref[k] = row_weights(jc_ref[k], width, even, sign)
@@ -294,9 +294,9 @@
     first, second, channels, _, wide = coherency.shape
     width = wide // 8
     lanes = wide // 2
-    block = 16
-    tile = 16
-    parts = 4
+    block = 8
+    tile = min(32, second // 2)
+    parts = 1
     slots = 4
     depth = 16 * channels
     f32, bf16 = jnp.float32, jnp.bfloat16
@@ -387,20 +387,23 @@
 
 
 def spread_kernel(
-    row_total, col_total, holders_ref, send_ref, row_ref, col_ref,
-    recv_ref, x_send, x_recv, c_send, c_recv, a_send, a_recv, b_send, b_recv,
+    row_total, col_total, table_ref, sent_ref, row_ref, col_ref,
+    send_ref, load_sem, recv_ref, x_send, x_recv, c_send, c_recv, a_send, a_recv, b_send, b_recv,
 ):
-    share = holders_ref.shape[1]
+    share = row_ref.shape[0] // col_total
     r = lax.axis_index("row")
     c = lax.axis_index("col")
     total = row_total * col_total
     me = r * col_total + c
+    load = pltpu.make_async_copy(sent_ref, send_ref, load_sem.at[0])
+    load.start()
     greet(me, total, col_total)
+    load.wait()
     exchange(send_ref, recv_ref, x_send, x_recv, me, total, col_total)
 
     def choose(j):
-        row_ref[c * share + j] = recv_ref[holders_ref[0, j], 0]
-        col_ref[r * share + j] = recv_ref[holders_ref[1, j], 1]
+        row_ref[c * share + j] = recv_ref[table_ref[j], 0]
+        col_ref[r * share + j] = recv_ref[table_ref[share + j], 1]
 
     each(0, share, choose)
     half = col_total // 2
@@ -436,11 +439,11 @@
 
 
 def collect_kernel(
-    row_total, col_total, back_ref, own_ref, row_ref, col_ref, out_ref,
-    pair_ref, part_ref, far_ref, colin_ref, sums_ref, send_ref, recv_ref,
+    row_total, col_total, table_ref, rows_ref, cols_ref, out_ref,
+    row_ref, col_ref, load_sem, pair_ref, part_ref, far_ref, colin_ref, sums_ref, send_ref, recv_ref,
     x_send, x_recv, c_send, c_recv, a_send, a_recv, b_send, b_recv,
 ):
-    share = own_ref.shape[1]
+    share = out_ref.shape[0]
     r = lax.axis_index("row")
     c = lax.axis_index("col")
     total = row_total * col_total
@@ -448,7 +451,13 @@
     half = col_total // 2
     core = c % 2
     chip = c // 2
+    load_rows = pltpu.make_async_copy(rows_ref, row_ref, load_sem.at[0])
+    load_cols = pltpu.make_async_copy(cols_ref, col_ref, load_sem.at[1])
+    load_rows.start()
+    load_cols.start()
     greet(me, total, col_total)
+    load_rows.wait()
+    load_cols.wait()
 
     def near_copy(offset):
         q = lax.rem(chip + offset, half)
@@ -500,14 +509,14 @@
     each(0, half, lambda offset: near_copy(offset).wait_send())
 
     def address(place):
-        send_ref[place, 0] = sums_ref[0, back_ref[0, place]]
-        send_ref[place, 1] = sums_ref[1, back_ref[1, place]]
+        send_ref[place, 0] = sums_ref[0, table_ref[4 * share + place]]
+        send_ref[place, 1] = sums_ref[1, table_ref[4 * share + total + place]]
 
     each(0, total, address)
     exchange(send_ref, recv_ref, x_send, x_recv, me, total, col_total)
 
     def settle(j):
-        out_ref[j] = recv_ref[own_ref[0, j], 0] + recv_ref[own_ref[1, j], 1]
+        out_ref[j] = recv_ref[table_ref[2 * share + j], 0] + recv_ref[table_ref[3 * share + j], 1]
 
     each(0, share, settle)
 
@@ -546,36 +555,46 @@
     col_block = col_place * row_total + row_place
     row_holder = lax.dynamic_slice_in_dim(station_slot, device_place * share, share) // share
     col_holder = lax.dynamic_slice_in_dim(station_slot, col_block * share, share) // share
-    holders = jnp.stack([row_holder, col_holder])
-    targets = jnp.stack([own_blocks, col_target])
+    numbers = jnp.concatenate(
+        [
+            row_holder,
+            col_holder,
+            own_blocks,
+            col_target,
+            places(row_holder, groups),
+            places(col_holder, groups),
+        ]
+    )
     picks = jnp.stack([places(own_blocks, groups), places(col_target, groups)], axis=1)
-    sent = jnp.take(gains, picks.reshape(-1), axis=0).reshape((groups, 2) + tail)
+    sent = jnp.take(gains, picks.reshape(-1), axis=0, mode="clip").reshape((groups, 2) + tail)
     vmem = pl.BlockSpec(memory_space=pltpu.VMEM)
     smem = pl.BlockSpec(memory_space=pltpu.SMEM)
     f32 = jnp.float32
     table = pltpu.VMEM((groups, 2) + tail, f32)
     row_gains, col_gains = pl.pallas_call(
         functools.partial(spread_kernel, row_total, col_total),
-        in_specs=[smem, vmem],
+        in_specs=[smem, pl.BlockSpec(memory_space=pl.ANY)],
         out_specs=[vmem, vmem],
         out_shape=[
             jax.ShapeDtypeStruct((col_total * share,) + tail, f32),
             jax.ShapeDtypeStruct((row_total * share,) + tail, f32),
         ],
-        scratch_shapes=[table] + semaphores(groups, row_total, col_total),
+        scratch_shapes=[table, pltpu.SemaphoreType.DMA((1,)), table] + semaphores(groups, row_total, col_total),
         compiler_params=call_options(1),
-    )(holders, sent)
+    )(numbers, sent)
     row_side, col_side = block_gradients(
         coherency, residuals(cotangent, flags), row_gains, col_gains
     )
-    backs = jnp.stack([places(row_holder, groups), places(col_holder, groups)])
     half = col_total // 2
     return pl.pallas_call(
         functools.partial(collect_kernel, row_total, col_total),
-        in_specs=[smem, smem, vmem, vmem],
+        in_specs=[smem] + [pl.BlockSpec(memory_space=pl.ANY)] * 2,
         out_specs=vmem,
         out_shape=jax.ShapeDtypeStruct(gains.shape, f32),
         scratch_shapes=[
+            pltpu.VMEM(row_side.shape, f32),
+            pltpu.VMEM(col_side.shape, f32),
+            pltpu.SemaphoreType.DMA((2,)),
             pltpu.VMEM((half, share) + tail, f32),
             pltpu.VMEM((half, share) + tail, f32),
             pltpu.VMEM((half, share) + tail, f32),
@@ -586,7 +605,7 @@
         ]
         + semaphores(groups, row_total, col_total),
         compiler_params=call_options(2),
-    )(backs, targets, row_side, col_side)
+    )(numbers, row_side, col_side)
 
 
 def solution(mesh):

time: 151 us -> 143 us (0.947)
  Pallas kernels: 142 us -> 135 us
    pallas_call x1, Pallas kernels: 73.2 us -> 66.7 us  [block_gradients(): pl.pallas_call(functools.partial(gradient_kernel, width, block, tile, par...]
    another operation x3 -> x0, other arithmetic: 1.69 us -> none  [the longest x1 0.57 us: shards(): holders = jnp.stack([row_holder, col_holder])]
where the time goes in v2:
time: 143 us
  Pallas kernels  135 us (94%)
  other arithmetic  4.49 us (3%)
  local copies, waits for them, and re-layouts  3.78 us (3%)
    pallas_call x1, Pallas kernels, block_gradients(): pl.pallas_call(functools.partial(gradient_kernel, width, block, tile, par...  66.7 us
    pallas_call x1, Pallas kernels, shards(): pl.pallas_call(functools.partial(spread_kernel, row_total, col_total), in...  35.1 us
    pallas_call x1, Pallas kernels, shards(): pl.pallas_call(functools.partial(collect_kernel, row_total, col_total), i...  32.9 us

profile of v2, /device:TPU:0, one launch (start us, length us, event | category | flops | bytes accessed | tf_op | source)
XLA Modules:
  0.0 143.0 jit_solution(7015607111594713558)
XLA Ops:
  0.0 0.0 copy-start
  0.0 0.0 copy-start.1
  0.0 1.0 select_reduce_fusion
  1.0 0.8 and_select_fusion.3
  1.8 0.1 select_reduce_fusion.1
  1.9 0.1 select_reduce_fusion.3
  2.0 0.6 concatenate.3.table_ref
  2.6 0.1 copy.8
  2.7 0.1 reshape.78
  2.8 0.8 convert_element_type.11
  3.6 0.0 copy-done
  3.6 1.4 gather_fusion
  5.0 35.1 %shard_map.55 = (f32[128,8,256]{2,1,0:T(8,128)}, f32[64,8,256]{2,1,0:T(8,128)}) custom-call(s32[128]{0:T(128)} %concatenate.3.table_ref, f32[32,2,8,256]{3,2,1,0:T(8,128)} %bitcast.17), custom_call_target="tpu_custom_call" | custom-call | tf_op jit(solution)/shard_map/pallas_call | solution.py:574
  40.1 0.0 copy-done.1
  40.1 1.7 %fusion.g_ref = f32[64,64,128]{2,1,0:T(8,128)} fusion(bf16[128,64,8,1,8]{0,4,3,2,1:T(8,128)(2,1)S(1)} %copy-done.1, f32[128,64]{0,1:T(8,128)S(1)} %bitcast.18), kind=kLoop, calls=%fused_computation.2 | loop fusion | flops 1048576 | bytes 3178496 | tf_op jit(solution)/shard_map/reshape | solution.py:290
  41.8 66.7 %shard_map.56 = (f32[128,8,256]{2,1,0:T(8,128)}, f32[64,8,256]{2,1,0:T(8,128)}) custom-call(bf16[128,64,16,128]{3,2,1,0:T(8,128)(2,1)} %bitcast.16, f32[64,64,128]{2,1,0:T(8,128)} %fusion.g_ref, f32[128,8,256]{2,1,0:T(8,128)} %get-tuple-element.9.jr_ref, f32[64,8,256]{2,1,0:T(8,128)} %get-tuple-element.10.jc_ref), custom_call_target="tpu_custom_call" | custom-call | tf_op jit(solution)/shard_map/pallas_call | solution.py:310
  108.5 32.9 %shard_map.57 = f32[16,8,256]{2,1,0:T(8,128)} custom-call(s32[128]{0:T(128)} %concatenate.3.table_ref, f32[128,8,256]{2,1,0:T(8,128)} %get-tuple-element.11.rows_ref, f32[64,8,256]{2,1,0:T(8,128)} %get-tuple-element.12.cols_ref), custom_call_target="tpu_custom_call" | custom-call | tf_op jit(solution)/shard_map/pallas_call | solution.py:589
  141.5 1.6 %copy.10 = f32[16,8,256]{2,1,0:T(8,128)} copy(f32[16,8,256]{2,1,0:T(8,128)} %shard_map.57) | data formatting | bytes 262144
  (4 shorter events, 0.0 us)
Async XLA Ops:
  0.0 3.6 %copy-start = (f32[16,8,256]{2,1,0:T(8,128)S(1)}, f32[16,8,256]{2,1,0:T(8,128)}, u32[]{:S(2)}) copy-start(f32[16,8,256]{2,1,0:T(8,128)} %param.5) | copy-start | bytes 393220
  0.0 40.1 %copy-start.1 = (bf16[128,64,8,1,8]{0,4,3,2,1:T(8,128)(2,1)S(1)}, bf16[128,64,8,1,8]{0,4,3,2,1:T(8,128)(2,1)}, u32[]{:S(2)}) copy-start(bf16[128,64,8,1,8]{0,4,3,2,1:T(8,128)(2,1)} %param.7) | copy-start | bytes 3145732

commit v3 on v2

--- a/solution.py
+++ b/solution.py
@@ -383,12 +383,13 @@
 
     each(1, total, lambda offset: copy(offset).start())
     recv_ref[me] = send_ref[me]
-    each(1, total, lambda offset: copy(offset).wait())
+    return lambda: each(1, total, lambda offset: copy(offset).wait())
 
 
 def spread_kernel(
     row_total, col_total, table_ref, sent_ref, row_ref, col_ref,
-    send_ref, load_sem, recv_ref, x_send, x_recv, c_send, c_recv, a_send, a_recv, b_send, b_recv,
+    send_ref, load_sem, recv_row_ref, recv_col_ref,
+    x_send, x_recv, y_send, y_recv, c_send, c_recv, a_send, a_recv, b_send, b_recv,
 ):
     share = row_ref.shape[0] // col_total
     r = lax.axis_index("row")
@@ -399,13 +400,21 @@
     load.start()
     greet(me, total, col_total)
     load.wait()
-    exchange(send_ref, recv_ref, x_send, x_recv, me, total, col_total)
-
-    def choose(j):
-        row_ref[c * share + j] = recv_ref[table_ref[j], 0]
-        col_ref[r * share + j] = recv_ref[table_ref[share + j], 1]
-
-    each(0, share, choose)
+    row_done = exchange(
+        send_ref.at[0], recv_row_ref, x_send, x_recv, me, total, col_total
+    )
+    col_done = exchange(
+        send_ref.at[1], recv_col_ref, y_send, y_recv, me, total, col_total
+    )
+    row_done()
+
+    def choose_row(j):
+        row_ref[c * share + j] = recv_row_ref[table_ref[j]]
+
+    def choose_col(j):
+        col_ref[r * share + j] = recv_col_ref[table_ref[share + j]]
+
+    each(0, share, choose_row)
     half = col_total // 2
     partner = c + 1 - 2 * (c % 2)
 
@@ -425,8 +434,10 @@
         return remote(block, block, b_send.at[offset], b_recv.at[offset], (r, partner))
 
     each(1, half, lambda offset: far_copy(offset).start())
+    near_copy(0).start()
+    col_done()
+    each(0, share, choose_col)
     each(1, row_total, lambda offset: col_copy(offset).start())
-    near_copy(0).start()
 
     def forward(offset):
         far_copy(offset).wait_recv()
@@ -440,8 +451,9 @@
 
 def collect_kernel(
     row_total, col_total, table_ref, rows_ref, cols_ref, out_ref,
-    row_ref, col_ref, load_sem, pair_ref, part_ref, far_ref, colin_ref, sums_ref, send_ref, recv_ref,
-    x_send, x_recv, c_send, c_recv, a_send, a_recv, b_send, b_recv,
+    row_ref, col_ref, load_sem, pair_ref, part_ref, far_ref, colin_ref, row_sum_ref, col_sum_ref,
+    send_row_ref, send_col_ref, recv_row_ref, recv_col_ref,
+    x_send, x_recv, y_send, y_recv, c_send, c_recv, a_send, a_recv, b_send, b_recv,
 ):
     share = out_ref.shape[0]
     r = lax.axis_index("row")
@@ -493,36 +505,43 @@
     each(1, row_total, lambda offset: col_copy(offset).start())
     each(1, half, join_and_send)
     join(0)
-    sums_ref[0] = part_ref[chip]
-    sums_ref[1] = col_ref[pl.ds(r * share, share)]
+    col_sum_ref[...] = col_ref[pl.ds(r * share, share)]
 
     def add_col(offset):
         col_copy(offset).wait()
-        sums_ref[1] += colin_ref[offset]
+        col_sum_ref[...] += colin_ref[offset]
 
     def add_row(offset):
         far_copy(offset).wait()
-        sums_ref[0] += far_ref[offset]
+        row_sum_ref[...] += far_ref[offset]
+
+    def address_col(place):
+        send_col_ref[place] = col_sum_ref[table_ref[4 * share + total + place]]
+
+    def address_row(place):
+        send_row_ref[place] = row_sum_ref[table_ref[4 * share + place]]
 
     each(1, row_total, add_col)
+    each(0, total, address_col)
+    col_done = exchange(send_col_ref, recv_col_ref, y_send, y_recv, me, total, col_total)
+    row_sum_ref[...] = part_ref[chip]
     each(1, half, add_row)
     each(0, half, lambda offset: near_copy(offset).wait_send())
-
-    def address(place):
-        send_ref[place, 0] = sums_ref[0, table_ref[4 * share + place]]
-        send_ref[place, 1] = sums_ref[1, table_ref[4 * share + total + place]]
-
-    each(0, total, address)
-    exchange(send_ref, recv_ref, x_send, x_recv, me, total, col_total)
+    each(0, total, address_row)
+    row_done = exchange(send_row_ref, recv_row_ref, x_send, x_recv, me, total, col_total)
+    col_done()
+    row_done()
 
     def settle(j):
-        out_ref[j] = recv_ref[table_ref[2 * share + j], 0] + recv_ref[table_ref[3 * share + j], 1]
+        out_ref[j] = (
+            recv_row_ref[table_ref[2 * share + j]] + recv_col_ref[table_ref[3 * share + j]]
+        )
 
     each(0, share, settle)
 
 
 def semaphores(total, row_total, col_total):
-    counts = (total, row_total, col_total // 2, col_total // 2)
+    counts = (total, total, row_total, col_total // 2, col_total // 2)
     return [pltpu.SemaphoreType.DMA((count,)) for count in counts for _ in range(2)]
 
 
@@ -565,12 +584,12 @@
             places(col_holder, groups),
         ]
     )
-    picks = jnp.stack([places(own_blocks, groups), places(col_target, groups)], axis=1)
-    sent = jnp.take(gains, picks.reshape(-1), axis=0, mode="clip").reshape((groups, 2) + tail)
+    picks = jnp.concatenate([places(own_blocks, groups), places(col_target, groups)])
+    sent = jnp.take(gains, picks, axis=0, mode="clip").reshape((2, groups) + tail)
     vmem = pl.BlockSpec(memory_space=pltpu.VMEM)
     smem = pl.BlockSpec(memory_space=pltpu.SMEM)
     f32 = jnp.float32
-    table = pltpu.VMEM((groups, 2) + tail, f32)
+    table = pltpu.VMEM((groups,) + tail, f32)
     row_gains, col_gains = pl.pallas_call(
         functools.partial(spread_kernel, row_total, col_total),
         in_specs=[smem, pl.BlockSpec(memory_space=pl.ANY)],
@@ -579,7 +598,13 @@
             jax.ShapeDtypeStruct((col_total * share,) + tail, f32),
             jax.ShapeDtypeStruct((row_total * share,) + tail, f32),
         ],
-        scratch_shapes=[table, pltpu.SemaphoreType.DMA((1,)), table] + semaphores(groups, row_total, col_total),
+        scratch_shapes=[
+            pltpu.VMEM((2, groups) + tail, f32),
+            pltpu.SemaphoreType.DMA((1,)),
+            table,
+            table,
+        ]
+        + semaphores(groups, row_total, col_total),
         compiler_params=call_options(1),
     )(numbers, sent)
     row_side, col_side = block_gradients(
@@ -599,7 +624,10 @@
             pltpu.VMEM((half, share) + tail, f32),
             pltpu.VMEM((half, share) + tail, f32),
             pltpu.VMEM((row_total, share) + tail, f32),
-            pltpu.VMEM((2, share) + tail, f32),
+            pltpu.VMEM((share,) + tail, f32),
+            pltpu.VMEM((share,) + tail, f32),
+            table,
+            table,
             table,
             table,
         ]

time: 143 us -> 141 us (0.986)
  Pallas kernels: 135 us -> 133 us
    pallas_call x1, Pallas kernels: 35.1 us -> 32.9 us  [shards(): pl.pallas_call(functools.partial(spread_kernel, row_total, col_total), in...]
where the time goes in v3:
time: 141 us
  Pallas kernels  133 us (94%)
  other arithmetic  4.55 us (3%)
  local copies, waits for them, and re-layouts  3.59 us (3%)
    pallas_call x1, Pallas kernels, block_gradients(): pl.pallas_call(functools.partial(gradient_kernel, width, block, tile, par...  66.7 us
    pallas_call x1, Pallas kernels, shards(): pl.pallas_call(functools.partial(collect_kernel, row_total, col_total), i...  33.4 us
    pallas_call x1, Pallas kernels, shards(): pl.pallas_call(functools.partial(spread_kernel, row_total, col_total), in...  32.9 us

profile of v3, /device:TPU:0, one launch (start us, length us, event | category | flops | bytes accessed | tf_op | source)
XLA Modules:
  0.0 141.2 jit_solution(8013203842453274547)
XLA Ops:
  0.0 0.0 copy-start
  0.0 0.0 copy-start.1
  0.0 1.0 select_reduce_fusion
  1.0 0.8 and_select_fusion.3
  1.8 0.1 select_reduce_fusion.1
  1.9 0.1 pad_add_fusion
  2.0 0.1 select_reduce_fusion.3
  2.1 0.6 concatenate.6.table_ref
  2.7 0.8 convert_element_type.11
  3.5 0.0 copy-done
  3.5 1.4 %gather_fusion = f32[64,8,256]{2,1,0:T(8,128)} fusion(f32[16,8,256]{2,1,0:T(8,128)S(1)} %copy-done, s32[1024]{0:T(1024)S(1)} %pad_clamp_fusion), kind=kCustom, calls=%fused_computation | custom fusion | bytes 1048832 | tf_op jit(solution)/shard_map/jit(_take)/gather | solution.py:588
  4.9 32.9 %shard_map.55 = (f32[128,8,256]{2,1,0:T(8,128)}, f32[64,8,256]{2,1,0:T(8,128)}) custom-call(s32[128]{0:T(128)} %concatenate.6.table_ref, f32[2,32,8,256]{3,2,1,0:T(8,128)} %bitcast.15), custom_call_target="tpu_custom_call" | custom-call | tf_op jit(solution)/shard_map/pallas_call | solution.py:593
  37.8 0.0 copy-done.1
  37.8 1.7 %fusion.g_ref = f32[64,64,128]{2,1,0:T(8,128)} fusion(bf16[128,64,8,1,8]{0,4,3,2,1:T(8,128)(2,1)S(1)} %copy-done.1, f32[128,64]{0,1:T(8,128)S(1)} %bitcast.16), kind=kLoop, calls=%fused_computation.2 | loop fusion | flops 1048576 | bytes 3178496 | tf_op jit(solution)/shard_map/reshape | solution.py:290
  39.5 66.7 %shard_map.56 = (f32[128,8,256]{2,1,0:T(8,128)}, f32[64,8,256]{2,1,0:T(8,128)}) custom-call(bf16[128,64,16,128]{3,2,1,0:T(8,128)(2,1)} %bitcast.14, f32[64,64,128]{2,1,0:T(8,128)} %fusion.g_ref, f32[128,8,256]{2,1,0:T(8,128)} %get-tuple-element.9.jr_ref, f32[64,8,256]{2,1,0:T(8,128)} %get-tuple-element.10.jc_ref), custom_call_target="tpu_custom_call" | custom-call | tf_op jit(solution)/shard_map/pallas_call | solution.py:310
  106.2 33.4 %shard_map.57 = f32[16,8,256]{2,1,0:T(8,128)} custom-call(s32[128]{0:T(128)} %concatenate.6.table_ref, f32[128,8,256]{2,1,0:T(8,128)} %get-tuple-element.11.rows_ref, f32[64,8,256]{2,1,0:T(8,128)} %get-tuple-element.12.cols_ref), custom_call_target="tpu_custom_call" | custom-call | tf_op jit(solution)/shard_map/pallas_call | solution.py:614
  139.6 1.6 %copy.7 = f32[16,8,256]{2,1,0:T(8,128)} copy(f32[16,8,256]{2,1,0:T(8,128)} %shard_map.57) | data formatting | bytes 262144
  (3 shorter events, 0.0 us)
Async XLA Ops:
  0.0 3.5 %copy-start = (f32[16,8,256]{2,1,0:T(8,128)S(1)}, f32[16,8,256]{2,1,0:T(8,128)}, u32[]{:S(2)}) copy-start(f32[16,8,256]{2,1,0:T(8,128)} %param.5) | copy-start | bytes 393220
  0.0 37.8 %copy-start.1 = (bf16[128,64,8,1,8]{0,4,3,2,1:T(8,128)(2,1)S(1)}, bf16[128,64,8,1,8]{0,4,3,2,1:T(8,128)(2,1)}, u32[]{:S(2)}) copy-start(bf16[128,64,8,1,8]{0,4,3,2,1:T(8,128)(2,1)} %param.7) | copy-start | bytes 3145732
